TPU v7x, 32 devices: a whole 2x2x4 slice. The times are simulated.
32 devices in a mesh: pipe: 4 (over z), expert: 4 (over y, x), tensor: 2 (over core).
Axes of the slice: x: 2, y: 2, z: 4, core: 2. Of those that a mesh axis runs over, the one named last changes fastest.
Arguments:
- inputs_prev: bfloat16 [4, 512, 3584], P('pipe', 'expert', 'tensor'), may hold values from -6 to 6
- cotangent_next: bfloat16 [4, 512, 3584], P('pipe', 'expert', 'tensor'), may hold values from -6 to 6
- saved_input: bfloat16 [4, 512, 3584], P('pipe', 'expert', 'tensor'), may hold values from -6 to 6
- expert_ids: int32 [2, 4, 512, 8], P(None, 'pipe', 'expert'), may hold values from 0 to 255, as said below
- keep_mask: int32 [2, 4, 512, 8], P(None, 'pipe', 'expert'), may hold values from 0 to 1, as said below
- slot_pos: int32 [2, 4, 512, 8], P(None, 'pipe', 'expert'), may hold values from 0 to 3, as said below
- weight_q: int32 [2, 4, 512, 8], P(None, 'pipe', 'expert'), may hold values from 1 to 4095
- gate_routed: bfloat16 [4, 4, 3584, 512], P('pipe', 'expert', None, 'tensor'), may hold values from -0.09375 to 0.09375
- up_routed: bfloat16 [4, 4, 3584, 512], P('pipe', 'expert', None, 'tensor'), may hold values from -0.09375 to 0.09375
- down_routed: bfloat16 [4, 4, 512, 3584], P('pipe', 'expert', 'tensor'), may hold values from -0.1875 to 0.1875
- gate_shared: bfloat16 [4, 3584, 1024], P('pipe', None, 'tensor'), may hold values from -0.09375 to 0.09375
- up_shared: bfloat16 [4, 3584, 1024], P('pipe', None, 'tensor'), may hold values from -0.09375 to 0.09375
- down_shared: bfloat16 [4, 1024, 3584], P('pipe', 'tensor'), may hold values from -0.1875 to 0.1875
Outputs:
- out_act: bfloat16 [4, 512, 3584], P('pipe', 'expert', 'tensor')
- in_grad: bfloat16 [4, 512, 3584], P('pipe', 'expert', 'tensor')
Inputs may be any that keep to these rules, and one draw needn't show every extreme that they name: `expert_ids`: each row names 8 different experts; in every section and micro-batch one expert below 2 is named by every row. `keep_mask`: 1 only where the expert named is below 2; in one block of 128 rows no expert has more than 4 kept choices, and in every section and micro-batch one expert has exactly 4 in every block. `slot_pos`: kept choices of one block naming the same expert hold different slots; 0 where keep_mask is 0.
All inputs are finite; a program needn't handle non-finite values.
Results may differ from a plain program's by a relative error of at most 0.005.
Values may be sent and summed in bfloat16 or wider, within the bound.
A program may use at most 64 MiB of HBM per device.

v0:
```python
import jax
import jax.numpy as jnp
from jax import lax
from jax.sharding import PartitionSpec as P


def passed_along(block, axis, distance):
    devices = range(lax.axis_size(axis))
    route = [((i - distance) % len(devices), i) for i in devices]
    return lax.ppermute(block, axis, route)


def swish(values):
    return values * jax.nn.sigmoid(values)


def swish_slope(values):
    logistic = jax.nn.sigmoid(values)
    return logistic * (1.0 + values * (1.0 - logistic))


def contract_last(left, right):
    return lax.dot_general(
        left, right, (((1,), (1,)), ((), ())), preferred_element_type=jnp.float32
    )


def slot_plan(choice_ids, kept_flags, slot_index, weight_levels, total_slots, capacity):
    target = jnp.where(kept_flags > 0, choice_ids * capacity + slot_index, -1)
    slots = jnp.arange(total_slots, dtype=jnp.int32)
    match = target[None] == slots[:, None, None]
    chosen = jnp.sum(match.astype(jnp.int32), axis=2)
    level = jnp.sum(jnp.where(match, weight_levels[None], 0), axis=2)
    return (chosen.astype(jnp.bfloat16), level)


def section_link(values, offset):
    return passed_along(values, "pipe", offset)


def select_rows(chosen, values):
    return jnp.dot(chosen, values, preferred_element_type=jnp.float32)


def split_level(level):
    high = (level // 64).astype(jnp.float32) / 64.0
    low = (level % 64).astype(jnp.float32) / 4096.0
    return (high.astype(jnp.bfloat16), low.astype(jnp.bfloat16))


def combine(factors, rows):
    return lax.dot_general(
        factors, rows, (((0,), (0,)), ((), ())), preferred_element_type=jnp.float32
    )


def other_sums(total, n_tensor):
    width = total.shape[1] // n_tensor
    me = lax.axis_index("tensor")
    mine = lax.dynamic_slice_in_dim(total, me * width, width, axis=1)
    for step in range(1, n_tensor):
        to = (me + step) % n_tensor
        piece = lax.dynamic_slice_in_dim(total, to * width, width, axis=1)
        mine = mine + passed_along(piece, "tensor", step)
    return mine


def expert_local(rows_in, rows_saved, rows_cot, gate_w, up_w, down_w):
    gate_pre = jnp.dot(rows_in, gate_w, preferred_element_type=jnp.float32)
    up_pre = jnp.dot(rows_in, up_w, preferred_element_type=jnp.float32)
    hidden = (swish(gate_pre) * up_pre).astype(jnp.bfloat16)
    result = jnp.dot(hidden, down_w, preferred_element_type=jnp.float32).astype(jnp.bfloat16)
    gate_back = jnp.dot(rows_saved, gate_w, preferred_element_type=jnp.float32)
    up_back = jnp.dot(rows_saved, up_w, preferred_element_type=jnp.float32)
    grad_hidden = contract_last(rows_cot, down_w)
    grad_gate = (grad_hidden * up_back * swish_slope(gate_back)).astype(jnp.bfloat16)
    grad_up = (grad_hidden * swish(gate_back)).astype(jnp.bfloat16)
    grad_rows = (contract_last(grad_gate, gate_w) + contract_last(grad_up, up_w)).astype(
        jnp.bfloat16
    )
    return (result, grad_rows)


def shared_pass(full_in, full_saved, full_cot, gate_w, up_w, down_w):
    gate_pre = jnp.dot(full_in, gate_w, preferred_element_type=jnp.float32)
    up_pre = jnp.dot(full_in, up_w, preferred_element_type=jnp.float32)
    hidden = (swish(gate_pre) * up_pre).astype(jnp.bfloat16)
    shared_out = jnp.dot(hidden, down_w, preferred_element_type=jnp.float32)
    gate_back = jnp.dot(full_saved, gate_w, preferred_element_type=jnp.float32)
    up_back = jnp.dot(full_saved, up_w, preferred_element_type=jnp.float32)
    grad_hidden = contract_last(full_cot, down_w)
    grad_gate = (grad_hidden * up_back * swish_slope(gate_back)).astype(jnp.bfloat16)
    grad_up = (grad_hidden * swish(gate_back)).astype(jnp.bfloat16)
    shared_grad = contract_last(grad_gate, gate_w) + contract_last(grad_up, up_w)
    return (shared_out, shared_grad)


def local(
    inputs_prev,
    cotangent_next,
    saved_input,
    expert_ids,
    keep_mask,
    slot_pos,
    weight_q,
    gate_routed,
    up_routed,
    down_routed,
    gate_shared,
    up_shared,
    down_shared,
):
    capacity = inputs_prev.shape[1] // 32
    n_expert = lax.axis_size("expert")
    n_tensor = lax.axis_size("tensor")
    experts_here = n_expert // 2
    slots = experts_here * capacity
    forward_in = section_link(inputs_prev[0], 1)
    backward_in = section_link(cotangent_next[0], -1)
    chosen_f, level_f = slot_plan(
        expert_ids[0, 0], keep_mask[0, 0], slot_pos[0, 0], weight_q[0, 0], slots, capacity
    )
    chosen_b, level_b = slot_plan(
        expert_ids[1, 0], keep_mask[1, 0], slot_pos[1, 0], weight_q[1, 0], slots, capacity
    )
    gate_w = gate_routed[0, 0]
    up_w = up_routed[0, 0]
    down_w = down_routed[0, 0]
    full_saved = lax.all_gather(saved_input[0], "tensor", axis=1, tiled=True)
    full_in = lax.all_gather(forward_in, "tensor", axis=1, tiled=True)
    full_cot = lax.all_gather(backward_in, "tensor", axis=1, tiled=True)
    feature_count = full_in.shape[1]
    weight_b = jnp.sum(level_b, axis=1).astype(jnp.float32) / 4096.0
    parcel = jnp.stack(
        (
            select_rows(chosen_f, full_in).astype(jnp.bfloat16),
            select_rows(chosen_b, full_saved).astype(jnp.bfloat16),
            (weight_b[:, None] * select_rows(chosen_b, full_cot)).astype(jnp.bfloat16),
        )
    ).reshape(3, experts_here, 1, capacity, feature_count)
    parcel = jnp.broadcast_to(parcel, (3, experts_here, 2, capacity, feature_count))
    parcel = parcel.reshape(3, n_expert, capacity, feature_count)
    pieces = lax.all_to_all(parcel, "expert", split_axis=1, concat_axis=1, tiled=True)
    rows = pieces.reshape(3, n_expert * capacity, feature_count)
    result, grad_rows = expert_local(rows[0], rows[1], rows[2], gate_w, up_w, down_w)
    returned = lax.all_to_all(
        jnp.stack((result, grad_rows)).reshape(2, n_expert, capacity, feature_count),
        "expert",
        split_axis=1,
        concat_axis=1,
        tiled=True,
    )
    back = returned.reshape(2, n_expert * capacity, feature_count)

    def doubled(factors):
        spread = factors.reshape(experts_here, 1, capacity, -1)
        spread = jnp.broadcast_to(spread, (experts_here, 2) + spread.shape[2:])
        return spread.reshape(n_expert * capacity, -1)

    high_f, low_f = split_level(level_f)
    factors_f = jnp.concatenate((doubled(high_f), doubled(low_f)), axis=0)
    routed_out = combine(factors_f, jnp.concatenate((back[0], back[0]), axis=0))
    routed_grad = combine(doubled(chosen_b), back[1])
    shared_out, shared_grad = shared_pass(
        full_in, full_saved, full_cot, gate_shared[0], up_shared[0], down_shared[0]
    )
    summed_out = other_sums(routed_out + shared_out, n_tensor)
    summed_grad = other_sums(routed_grad + shared_grad, n_tensor)
    return (summed_out.astype(jnp.bfloat16)[None], summed_grad.astype(jnp.bfloat16)[None])


def solution(mesh):
    return jax.shard_map(
        local,
        mesh=mesh,
        in_specs=(
            P("pipe", "expert", "tensor"),
            P("pipe", "expert", "tensor"),
            P("pipe", "expert", "tensor"),
            P(None, "pipe", "expert", None),
            P(None, "pipe", "expert", None),
            P(None, "pipe", "expert", None),
            P(None, "pipe", "expert", None),
            P("pipe", "expert", None, "tensor"),
            P("pipe", "expert", None, "tensor"),
            P("pipe", "expert", "tensor", None),
            P("pipe", None, "tensor"),
            P("pipe", None, "tensor"),
            P("pipe", "tensor", None),
        ),
        out_specs=(P("pipe", "expert", "tensor"), P("pipe", "expert", "tensor")),
        check_vma=False,
    )
```

profile of v0, /device:TPU:0, one launch (start us, length us, event | category | flops | bytes accessed | tf_op | source)
XLA Modules:
  0.0 99.7 jit_solution(14145739943017148776)
XLA Ops:
  0.6 5.1 %collective-permute-start.1 = (bf16[128,1792]{1,0:T(8,128)(2,1)}, bf16[128,1792]{1,0:T(8,128)(2,1)}, u32[]{:S(2)}, u32[]{:S(2)}) collective-permute-start(bf16[128,1792]{1,0:T(8,128)(2,1)} %bitcast.127), channel_id=1, source_target_pairs={{8,0},{16,8},{24,16},{0,24},{9,1},{17,9},{25,17},{1,25},{10,2},{18... | collective-permute-start | bytes 1376264 | tf_op jit(solution)/shard_map/ppermute | solution.py:10
  6.8 2.7 %all-gather = bf16[1,128,3584]{2,1,0:T(8,128)(2,1)S(1)} all-gather(bf16[1,128,1792]{2,1,0:T(8,128)(2,1)} %param.15), channel_id=2, replica_groups=mesh['pipe'=4,'expert'=4,'tensor'=2] {'tensor'}, dimensions={2}, use_global_device_ids=true | all-gather | bytes 1376256 | tf_op jit(solution)/shard_map/all_gather | solution.py:129
  9.8 2.7 %fusion.13 = f32[128,512]{1,0:T(8,128)S(1)} fusion(bf16[1,3584,512]{2,1,0:T(8,128)(2,1)} %param.23, bf16[1,128,3584]{2,1,0:T(8,128)(2,1)S(1)} %all-gather), kind=kOutput, calls=%fused_computation.20 | convolution fusion | flops 469762048 | bytes 4849664 | tf_op jit(solution)/shard_map/dot_general | solution.py:89
  12.5 4.5 %collective-permute-done.1 = bf16[128,1792]{1,0:T(8,128)(2,1)} collective-permute-done((bf16[128,1792]{1,0:T(8,128)(2,1)}, bf16[128,1792]{1,0:T(8,128)(2,1)}, u32[]{:S(2)}, u32[]{:S(2)}) %collective-permute-start.1) | collective-permute-done | bytes 458784 | tf_op jit(solution)/shard_map/ppermute | solution.py:10
  17.0 2.7 %all_gather.11 = bf16[128,3584]{1,0:T(8,128)(2,1)S(1)} all-gather(bf16[128,1792]{1,0:T(8,128)(2,1)} %collective-permute-done.1), channel_id=1, replica_groups=mesh['pipe'=4,'expert'=4,'tensor'=2] {'tensor'}, dimensions={1}, use_global_device_ids=true | all-gather | bytes 1376256 | tf_op jit(solution)/shard_map/all_gather | solution.py:131
  20.6 1.5 %stack.23 = bf16[1,2,1,4,3584]{4,3,1,2,0:T(4,128)(2,1)} reshape(bf16[8,3584]{1,0:T(8,128)(2,1)} %fusion.2) | data formatting | bytes 114688 | tf_op jit(solution)/shard_map/stack | solution.py:134
  22.1 4.4 %collective-permute-done = bf16[128,1792]{1,0:T(8,128)(2,1)S(1)} collective-permute-done((bf16[128,1792]{1,0:T(8,128)(2,1)}, bf16[128,1792]{1,0:T(8,128)(2,1)S(1)}, u32[]{:S(2)}, u32[]{:S(2)}) %collective-permute-start) | collective-permute-done | bytes 458784 | tf_op jit(solution)/shard_map/ppermute | solution.py:10
  26.5 2.5 %all_gather.9 = bf16[128,3584]{1,0:T(8,128)(2,1)S(1)} all-gather(bf16[128,1792]{1,0:T(8,128)(2,1)S(1)} %collective-permute-done), channel_id=1, replica_groups=mesh['pipe'=4,'expert'=4,'tensor'=2] {'tensor'}, dimensions={1}, use_global_device_ids=true | all-gather | bytes 1376256 | tf_op jit(solution)/shard_map/all_gather | solution.py:130
  29.2 1.0 maximum_bitcast_fusion
  31.1 4.1 %all-to-all-start = ((bf16[3,4,4,3584]{3,2,0,1:T(4,128)(2,1)}), bf16[3,4,4,3584]{3,2,0,1:T(4,128)(2,1)}, u32[]{:S(2)}, u32[]{:S(2)}) async-start(bf16[3,4,4,3584]{3,2,0,1:T(4,128)(2,1)} %bitcast.11), calls=%async_computation | async-start | bytes 688128 | tf_op jit(solution)/shard_map/all_to_all | solution.py:143
  35.2 3.6 %fusion.3 = f32[128,512]{1,0:T(8,128)S(1)} fusion(bf16[128,3584]{1,0:T(8,128)(2,1)} %copy-done.3, bf16[1,512,3584]{2,1,0:T(8,128)(2,1)} %param.25), kind=kOutput, calls=%fused_computation.10 | convolution fusion | flops 469762048 | bytes 4849664 | tf_op jit(solution)/shard_map/dot_general | solution.py:23
  38.8 6.6 %fusion.11 = f32[128,3584]{1,0:T(8,128)} fusion(bf16[1,3584,512]{2,1,0:T(8,128)(2,1)} %param.23, f32[128,512]{1,0:T(8,128)S(1)} %fusion.3, bf16[1,3584,512]{2,1,0:T(8,128)(2,1)} %param.24, bf16[1,128,3584]{2,1,0:T(8,128)(2,1)} %copy-done.2, f32[128,512]{1,0:T(8,128)S(1)} %fusion.13), kind=kOutput, calls=%fused_computation.18 | convolution fusion | flops 940179456 | bytes 10616832 | tf_op jit(solution)/shard_map/dot_general | solution.py:23
  45.4 1.8 %fusion.112 = (bf16[1,4,4,3584]{3,2,0,1:T(4,128)(2,1)}, bf16[1,4,4,3584]{3,2,0,1:T(4,128)(2,1)S(1)}, bf16[1,4,4,3584]{3,2,0,1:T(4,128)(2,1)S(1)}) fusion(bf16[3,4,4,3584]{3,2,0,1:T(4,128)(2,1)} %all-to-all-done), kind=kLoop, calls=%fused_computation.123 | loop fusion | bytes 688128 | tf_op jit(solution)/shard_map/slice | solution.py:145
  47.9 2.2 %fusion.17 = f32[16,256]{1,0:T(8,128)S(1)} fusion(bf16[16,3584]{1,0:T(8,128)(2,1)} %squeeze.56, bf16[1,1,256,3584]{3,2,1,0:T(8,128)(2,1)} %param.22), kind=kOutput, calls=%fused_computation.24 | convolution fusion | flops 29360128 | bytes 1966080 | tf_op jit(solution)/shard_map/dot_general | solution.py:23
  50.5 3.5 %fusion.25 = f32[16,3584]{1,0:T(8,128)} fusion(bf16[1,1,3584,256]{3,2,1,0:T(8,128)(2,1)} %param.20, f32[16,256]{1,0:T(8,128)S(1)} %fusion.17, bf16[16,3584]{1,0:T(8,128)(2,1)S(1)} %squeeze.57, bf16[1,1,3584,256]{3,2,1,0:T(8,128)(2,1)S(1)} %copy-done, f32[16,256]{1,0:T(8,128)S(1)} %fusion.27), kind=kOutput, calls=%fused_computation.32 | convolution fusion | flops 58761216 | bytes 4046848 | tf_op jit(solution)/shard_map/dot_general | solution.py:23
  54.0 1.5 %fusion.1 = bf16[16,3584]{1,0:T(8,128)(2,1)S(1)} fusion(f32[16,3584]{1,0:T(8,128)} %fusion.25, bf16[1,1,3584,256]{3,2,1,0:T(8,128)(2,1)S(1)} %copy-done, f32[16,256]{1,0:T(8,128)S(1)} %fusion.17, f32[16,256]{1,0:T(8,128)S(1)} %fusion.27), kind=kOutput, calls=%fused_computation.4 | convolution fusion | flops 29499392 | bytes 2211840 | tf_op jit(solution)/shard_map/dot_general | solution.py:23
  56.5 1.8 %fusion.29 = f32[16,256]{1,0:T(8,128)S(1)} fusion(bf16[16,3584]{1,0:T(8,128)(2,1)S(1)} %squeeze.52, bf16[1,1,3584,256]{3,2,1,0:T(8,128)(2,1)} %param.20), kind=kOutput, calls=%fused_computation.36 | convolution fusion | flops 29360128 | bytes 1966080 | tf_op jit(solution)/shard_map/dot_general | solution.py:69
  58.3 3.3 %convolution_convert_fusion = bf16[16,3584]{1,0:T(8,128)(2,1)} fusion(bf16[1,1,256,3584]{3,2,1,0:T(8,128)(2,1)} %param.22, bf16[16,3584]{1,0:T(8,128)(2,1)S(1)} %squeeze.52, bf16[1,1,3584,256]{3,2,1,0:T(8,128)(2,1)S(1)} %copy-done, f32[16,256]{1,0:T(8,128)S(1)} %fusion.29), kind=kOutput, calls=%fused_computation.5 | convolution fusion | flops 58802176 | bytes 3915776 | tf_op jit(solution)/shard_map/dot_general | solution.py:72
  63.4 4.1 %all-to-all-start.1 = ((bf16[2,4,4,3584]{3,2,0,1:T(4,128)(2,1)}), bf16[2,4,4,3584]{3,2,0,1:T(4,128)(2,1)}, u32[]{:S(2)}, u32[]{:S(2)}) async-start(bf16[2,4,4,3584]{3,2,0,1:T(4,128)(2,1)} %pad_maximum_fusion), calls=%async_computation.1 | async-start | bytes 458752 | tf_op jit(solution)/shard_map/all_to_all | solution.py:146
  67.5 2.7 %fusion.9 = f32[128,512]{1,0:T(8,128)S(1)} fusion(bf16[128,3584]{1,0:T(8,128)(2,1)S(1)} %all_gather.9, bf16[1,3584,512]{2,1,0:T(8,128)(2,1)} %param.24), kind=kOutput, calls=%fused_computation.16 | convolution fusion | flops 469762048 | bytes 4849664 | tf_op jit(solution)/shard_map/dot_general | solution.py:86
  70.2 3.0 %all-to-all-done.1 = bf16[2,4,4,3584]{3,2,0,1:T(4,128)(2,1)} async-done(((bf16[2,4,4,3584]{3,2,0,1:T(4,128)(2,1)}), bf16[2,4,4,3584]{3,2,0,1:T(4,128)(2,1)}, u32[]{:S(2)}, u32[]{:S(2)}) %all-to-all-start.1) | async-done | bytes 229408 | tf_op jit(solution)/shard_map/all_to_all | solution.py:146
  73.2 1.7 %fusion.113 = (bf16[1,4,4,3584]{3,2,0,1:T(4,128)(2,1)}, bf16[1,4,4,3584]{3,2,0,1:T(4,128)(2,1)}) fusion(bf16[2,4,4,3584]{3,2,0,1:T(4,128)(2,1)} %all-to-all-done.1), kind=kLoop, calls=%fused_computation.124 | loop fusion | bytes 458752 | tf_op jit(solution)/shard_map/slice | solution.py:163
  74.9 1.6 %squeeze.58 = bf16[16,3584]{1,0:T(8,128)(2,1)} reshape(bf16[1,4,4,3584]{3,2,0,1:T(4,128)(2,1)} %get-tuple-element.10) | data formatting | bytes 229376 | tf_op jit(solution)/shard_map/squeeze | solution.py:162
  76.5 2.6 %fusion.71 = f32[128,3584]{1,0:T(8,128)} fusion(bf16[16,3584]{1,0:T(8,128)(2,1)} %squeeze.58, bf16[16,128]{1,0:T(8,128)(2,1)S(1)} %bitcast.123, bf16[16,128]{1,0:T(8,128)(2,1)S(1)} %bitcast.124), kind=kOutput, calls=%fused_computation.61 | convolution fusion | flops 29835264 | bytes 1957888 | tf_op jit(solution)/shard_map/dot_general | solution.py:52
  79.1 6.2 %convolution_add_fusion.1 = f32[128,3584]{1,0:T(8,128)} fusion(f32[128,3584]{1,0:T(8,128)} %fusion.71, bf16[1,512,3584]{2,1,0:T(8,128)(2,1)} %param.25, f32[128,512]{1,0:T(8,128)S(1)} %fusion.9, bf16[128,3584]{1,0:T(8,128)(2,1)S(1)} %all_gather.9, bf16[1,3584,512]{2,1,0:T(8,128)(2,1)} %param.23), kind=kOutput, calls=%fused_computation.2 | convolution fusion | flops 940376064 | bytes 12189696 | tf_op jit(solution)/shard_map/dot_general | solution.py:88
  85.3 2.2 %constant_dynamic-slice_fusion = f32[128,1792]{1,0:T(8,128)} fusion(f32[128,3584]{1,0:T(8,128)} %convolution_add_fusion.1, s32[]{:T(128)S(6)} %select_n.74), kind=kLoop, calls=%fused_computation.113 | loop fusion | bytes 1835012 | tf_op jit(solution)/shard_map/dynamic_slice | solution.py:63
  88.0 1.1 %copy-done.6 = f32[128,3584]{1,0:T(8,128)S(1)} copy-done((f32[128,3584]{1,0:T(8,128)S(1)}, f32[128,3584]{1,0:T(8,128)}, u32[]{:S(2)}) %copy-start.6) | copy-done | bytes 1835032
  89.1 3.4 %fusion = f32[128,3584]{1,0:T(8,128)S(1)} fusion(f32[128,3584]{1,0:T(8,128)S(1)} %fusion.114, f32[128,3584]{1,0:T(8,128)S(1)} %copy-done.6, bf16[1,3584,512]{2,1,0:T(8,128)(2,1)} %param.24, f32[128,512]{1,0:T(8,128)S(1)} %fusion.3, f32[128,512]{1,0:T(8,128)S(1)} %fusion.13), kind=kOutput, calls=%fused_computation.1 | convolution fusion | flops 471072768 | bytes 9699328 | tf_op jit(solution)/shard_map/dot_general | solution.py:23
  92.5 1.3 %copy-done.4 = f32[128,3584]{1,0:T(8,128)} copy-done((f32[128,3584]{1,0:T(8,128)}, f32[128,3584]{1,0:T(8,128)S(1)}, u32[]{:S(2)}) %copy-start.4) | copy-done | bytes 1835032
  93.7 1.0 %constant_dynamic-slice_fusion.1 = f32[128,1792]{1,0:T(8,128)} fusion(f32[128,3584]{1,0:T(8,128)S(1)} %fusion, s32[]{:T(128)S(6)} %select_n.74), kind=kLoop, calls=%fused_computation.114 | loop fusion | bytes 1835012 | tf_op jit(solution)/shard_map/dynamic_slice | solution.py:63
  95.2 2.2 %fusion.65 = bf16[1,128,1792]{2,1,0:T(8,128)(2,1)} fusion(f32[128,1792]{1,0:T(8,128)S(1)} %collective-permute-done.2, f32[128,3584]{1,0:T(8,128)} %convolution_add_fusion.1, s32[]{:T(128)S(6)} %select_n.72), kind=kLoop, calls=%fused_computation.51 | loop fusion | flops 458752 | bytes 2293764 | tf_op jit(solution)/shard_map/broadcast_in_dim | solution.py:169
  97.7 2.0 %fusion.66 = bf16[1,128,1792]{2,1,0:T(8,128)(2,1)} fusion(f32[128,1792]{1,0:T(8,128)} %collective-permute-done.3, f32[128,3584]{1,0:T(8,128)S(1)} %copy-done.5, s32[]{:T(128)S(6)} %select_n.72), kind=kLoop, calls=%fused_computation.52 | loop fusion | flops 458752 | bytes 2293764 | tf_op jit(solution)/shard_map/broadcast_in_dim | solution.py:169
  (45 shorter events, 8.5 us)
Async XLA Ops:
  0.6 49.9 %copy-start = (bf16[1,1,3584,256]{3,2,1,0:T(8,128)(2,1)S(1)}, bf16[1,1,3584,256]{3,2,1,0:T(8,128)(2,1)}, u32[]{:S(2)}) copy-start(bf16[1,1,3584,256]{3,2,1,0:T(8,128)(2,1)} %param.21) | copy-start | bytes 5505028
  0.6 16.4 %collective-permute-start.1 = (bf16[128,1792]{1,0:T(8,128)(2,1)}, bf16[128,1792]{1,0:T(8,128)(2,1)}, u32[]{:S(2)}, u32[]{:S(2)}) collective-permute-start(bf16[128,1792]{1,0:T(8,128)(2,1)} %bitcast.127), channel_id=1, source_target_pairs={{8,0},{16,8},{24,16},{0,24},{9,1},{17,9},{25,17},{1,25},{10,2},{18... | collective-permute-start | bytes 1376264 | tf_op jit(solution)/shard_map/ppermute | solution.py:10
  5.8 20.7 %collective-permute-start = (bf16[128,1792]{1,0:T(8,128)(2,1)}, bf16[128,1792]{1,0:T(8,128)(2,1)S(1)}, u32[]{:S(2)}, u32[]{:S(2)}) collective-permute-start(bf16[128,1792]{1,0:T(8,128)(2,1)} %bitcast.128), channel_id=1, source_target_pairs={{24,0},{0,8},{8,16},{16,24},{25,1},{1,9},{9,17},{17,25},{26,2},{2,... | collective-permute-start | bytes 1376264 | tf_op jit(solution)/shard_map/ppermute | solution.py:10
  9.5 3.0 %copy-start.2 = (bf16[1,128,3584]{2,1,0:T(8,128)(2,1)}, bf16[1,128,3584]{2,1,0:T(8,128)(2,1)S(1)}, u32[]{:S(2)}) copy-start(bf16[1,128,3584]{2,1,0:T(8,128)(2,1)S(1)} %all-gather) | copy-start | bytes 2752516
  19.7 2.4 %copy-start.3 = (bf16[128,3584]{1,0:T(8,128)(2,1)}, bf16[128,3584]{1,0:T(8,128)(2,1)S(1)}, u32[]{:S(2)}) copy-start(bf16[128,3584]{1,0:T(8,128)(2,1)S(1)} %all_gather.11) | copy-start | bytes 2752516
  31.1 14.3 %all-to-all-start = ((bf16[3,4,4,3584]{3,2,0,1:T(4,128)(2,1)}), bf16[3,4,4,3584]{3,2,0,1:T(4,128)(2,1)}, u32[]{:S(2)}, u32[]{:S(2)}) async-start(bf16[3,4,4,3584]{3,2,0,1:T(4,128)(2,1)} %bitcast.11), calls=%async_computation | async-start | bytes 688128 | tf_op jit(solution)/shard_map/all_to_all | solution.py:143
  47.8 2.3 %copy-start.1 = (bf16[1,1,3584,256]{3,2,1,0:T(8,128)(2,1)S(1)}, bf16[1,1,3584,256]{3,2,1,0:T(8,128)(2,1)}, u32[]{:S(2)}) copy-start(bf16[1,1,3584,256]{3,2,1,0:T(8,128)(2,1)} %param.20) | copy-start | bytes 5505028
  63.4 9.8 %all-to-all-start.1 = ((bf16[2,4,4,3584]{3,2,0,1:T(4,128)(2,1)}), bf16[2,4,4,3584]{3,2,0,1:T(4,128)(2,1)}, u32[]{:S(2)}, u32[]{:S(2)}) async-start(bf16[2,4,4,3584]{3,2,0,1:T(4,128)(2,1)} %pad_maximum_fusion), calls=%async_computation.1 | async-start | bytes 458752 | tf_op jit(solution)/shard_map/all_to_all | solution.py:146
  85.3 2.2 %copy-start.7 = (bf16[1,4,4,3584]{3,2,0,1:T(4,128)(2,1)S(1)}, bf16[1,4,4,3584]{3,2,0,1:T(4,128)(2,1)}, u32[]{:S(2)}) copy-start(bf16[1,4,4,3584]{3,2,0,1:T(4,128)(2,1)} %get-tuple-element.9) | copy-start | bytes 344068
  87.5 7.7 %collective-permute-start.2 = (f32[128,1792]{1,0:T(8,128)}, f32[128,1792]{1,0:T(8,128)S(1)}, u32[]{:S(2)}, u32[]{:S(2)}) collective-permute-start(f32[128,1792]{1,0:T(8,128)} %constant_dynamic-slice_fusion), channel_id=1, source_target_pairs={{1,0},{0,1},{3,2},{2,3},{5,4},{4,5},{7,6},{6,7},{9,8},{8,9},{11,10... | collective-permute-start | bytes 2752520 | tf_op jit(solution)/shard_map/ppermute | solution.py:10
  87.6 1.5 %copy-start.6 = (f32[128,3584]{1,0:T(8,128)S(1)}, f32[128,3584]{1,0:T(8,128)}, u32[]{:S(2)}) copy-start(f32[128,3584]{1,0:T(8,128)} %fusion.11) | copy-start | bytes 5505028
  92.4 1.3 %copy-start.4 = (f32[128,3584]{1,0:T(8,128)}, f32[128,3584]{1,0:T(8,128)S(1)}, u32[]{:S(2)}) copy-start(f32[128,3584]{1,0:T(8,128)S(1)} %fusion) | copy-start | bytes 5505028
  94.7 2.9 %collective-permute-start.3 = (f32[128,1792]{1,0:T(8,128)}, f32[128,1792]{1,0:T(8,128)}, u32[]{:S(2)}, u32[]{:S(2)}) collective-permute-start(f32[128,1792]{1,0:T(8,128)} %constant_dynamic-slice_fusion.1), channel_id=1, source_target_pairs={{1,0},{0,1},{3,2},{2,3},{5,4},{4,5},{7,6},{6,7},{9,8},{8,9},{11,10... | collective-permute-start | bytes 2752520 | tf_op jit(solution)/shard_map/ppermute | solution.py:10
  95.2 2.4 %copy-start.5 = (f32[128,3584]{1,0:T(8,128)S(1)}, f32[128,3584]{1,0:T(8,128)}, u32[]{:S(2)}) copy-start(f32[128,3584]{1,0:T(8,128)} %copy-done.4) | copy-start | bytes 5505028
where the time goes:
time: 101 us; the launch traced here: 99.7 us
  matrix products  42.3 us (42%)
  local copies, waits for them, and re-layouts  15.7 us (16%)
  starting transfers between devices  13.9 us (14%)
  waiting for transfers between devices  12.2 us (12%)
  blocking collectives  7.79 us (8%)
  other arithmetic  7.08 us (7%)
    dot_general x6, matrix products, contract_last(): lax.dot_general(left, right, (((1,), (1,)), ((), ())), preferred_element_...  20.8 us
    ppermute x4, waiting for transfers between devices, passed_along(): return lax.ppermute(block, axis, route)  9.2 us
    dot_general x1, matrix products, shared_pass(): shared_out = jnp.dot(hidden, down_w, preferred_element_type=jnp.float32)  6.2 us
    ppermute x4, starting transfers between devices, passed_along(): return lax.ppermute(block, axis, route)  5.64 us
    all_to_all x1, starting transfers between devices, local(): lax.all_to_all(jnp.stack((result, grad_rows)).reshape(2, n_expert, capaci...  4.14 us
    all_to_all x1, starting transfers between devices, local(): lax.all_to_all(parcel, 'expert', split_axis=1, concat_axis=1, tiled=True)  4.1 us
    dot_general x1, matrix products, expert_local(): jnp.dot(hidden, down_w, preferred_element_type=jnp.float32)  3.3 us
    dynamic_slice x2, local copies, waits for them, and re-layouts, other_sums(): piece = lax.dynamic_slice_in_dim(total, to * width, width, axis=1)  3.22 us
  transfers between devices with their start and end apart: 6, of which 4 were waited for; matrix products, arithmetic and copies ran while one was open for 26% of the time, Pallas kernels for 0%

commit v1 on v0

--- a/solution.py
+++ b/solution.py
@@ -143,12 +143,20 @@
     pieces = lax.all_to_all(parcel, "expert", split_axis=1, concat_axis=1, tiled=True)
     rows = pieces.reshape(3, n_expert * capacity, feature_count)
     result, grad_rows = expert_local(rows[0], rows[1], rows[2], gate_w, up_w, down_w)
-    returned = lax.all_to_all(
-        jnp.stack((result, grad_rows)).reshape(2, n_expert, capacity, feature_count),
-        "expert",
-        split_axis=1,
-        concat_axis=1,
-        tiled=True,
+    returned = jnp.concatenate(
+        lax.all_to_all(
+            jnp.stack(
+                jnp.split(
+                    jnp.stack((result, grad_rows)).reshape(2, n_expert, capacity, feature_count),
+                    lax.axis_size("expert"),
+                    axis=1,
+                )
+            ),
+            "expert",
+            0,
+            0,
+        ),
+        axis=1,
     )
     back = returned.reshape(2, n_expert * capacity, feature_count)
 

time: 101 us -> 106 us (1.050)
  local copies, waits for them, and re-layouts: 15.7 us -> 19.4 us
  matrix products: 42.3 us -> 43.5 us
    another operation x2 -> x3, local copies, waits for them, and re-layouts: 0.97 us -> 3.46 us  [local(): jnp.stack((result, grad_rows)).reshape(2, n_expert, capacity, feature_count)]
    unnamed x16 -> x17, local copies, waits for them, and re-layouts: 2.35 us -> 3.95 us
    dot_general x1, matrix products: 0.38 us -> 1.85 us  [expert_local(): gate_back = jnp.dot(rows_saved, gate_w, preferred_element_type=jnp.float32)]
  transfers between devices with their start and end apart: 6 -> 6, of which waited for: 4 -> 4; matrix products, arithmetic and copies ran while one was open for 26% -> 23% of each run, Pallas kernels for 0% -> 0%
where the time goes in v1:
time: 106 us; the launch traced here: 105 us
  matrix products  43.5 us (41%)
  local copies, waits for them, and re-layouts  19.4 us (18%)
  starting transfers between devices  13.9 us (13%)
  waiting for transfers between devices  12.7 us (12%)
  blocking collectives  7.79 us (7%)
  other arithmetic  7.13 us (7%)
    dot_general x6, matrix products, contract_last(): lax.dot_general(left, right, (((1,), (1,)), ((), ())), preferred_element_...  21.3 us
    ppermute x4, waiting for transfers between devices, passed_along(): return lax.ppermute(block, axis, route)  9.78 us
    dot_general x1, matrix products, shared_pass(): shared_out = jnp.dot(hidden, down_w, preferred_element_type=jnp.float32)  6.19 us
    ppermute x4, starting transfers between devices, passed_along(): return lax.ppermute(block, axis, route)  5.65 us
    all_to_all x1, starting transfers between devices, local(): lax.all_to_all(jnp.stack(jnp.split(jnp.stack((result, grad_rows)).reshape...  4.14 us
    all_to_all x1, starting transfers between devices, local(): lax.all_to_all(parcel, 'expert', split_axis=1, concat_axis=1, tiled=True)  4.09 us
    unnamed x17, local copies, waits for them, and re-layouts  3.95 us
    another operation x3, local copies, waits for them, and re-layouts, local(): jnp.stack((result, grad_rows)).reshape(2, n_expert, capacity, feature_count)  3.46 us
  transfers between devices with their start and end apart: 6, of which 4 were waited for; matrix products, arithmetic and copies ran while one was open for 23% of the time, Pallas kernels for 0%

profile of v1, /device:TPU:0, one launch (start us, length us, event | category | flops | bytes accessed | tf_op | source)
XLA Modules:
  0.0 105.2 jit_solution(9961535169411248471)
XLA Ops:
  0.6 5.1 %collective-permute-start.1 = (bf16[128,1792]{1,0:T(8,128)(2,1)}, bf16[128,1792]{1,0:T(8,128)(2,1)}, u32[]{:S(2)}, u32[]{:S(2)}) collective-permute-start(bf16[128,1792]{1,0:T(8,128)(2,1)} %bitcast.138), channel_id=1, source_target_pairs={{8,0},{16,8},{24,16},{0,24},{9,1},{17,9},{25,17},{1,25},{10,2},{18... | collective-permute-start | bytes 1376264 | tf_op jit(solution)/shard_map/ppermute | solution.py:10
  6.8 2.7 %all-gather = bf16[1,128,3584]{2,1,0:T(8,128)(2,1)S(1)} all-gather(bf16[1,128,1792]{2,1,0:T(8,128)(2,1)} %param.15), channel_id=2, replica_groups=mesh['pipe'=4,'expert'=4,'tensor'=2] {'tensor'}, dimensions={2}, use_global_device_ids=true | all-gather | bytes 1376256 | tf_op jit(solution)/shard_map/all_gather | solution.py:129
  9.8 2.7 %fusion.13 = f32[128,512]{1,0:T(8,128)S(1)} fusion(bf16[1,3584,512]{2,1,0:T(8,128)(2,1)} %param.23, bf16[1,128,3584]{2,1,0:T(8,128)(2,1)S(1)} %all-gather), kind=kOutput, calls=%fused_computation.20 | convolution fusion | flops 469762048 | bytes 4849664 | tf_op jit(solution)/shard_map/dot_general | solution.py:89
  12.5 4.5 %collective-permute-done.1 = bf16[128,1792]{1,0:T(8,128)(2,1)} collective-permute-done((bf16[128,1792]{1,0:T(8,128)(2,1)}, bf16[128,1792]{1,0:T(8,128)(2,1)}, u32[]{:S(2)}, u32[]{:S(2)}) %collective-permute-start.1) | collective-permute-done | bytes 458784 | tf_op jit(solution)/shard_map/ppermute | solution.py:10
  17.0 2.7 %all_gather.11 = bf16[128,3584]{1,0:T(8,128)(2,1)S(1)} all-gather(bf16[128,1792]{1,0:T(8,128)(2,1)} %collective-permute-done.1), channel_id=1, replica_groups=mesh['pipe'=4,'expert'=4,'tensor'=2] {'tensor'}, dimensions={1}, use_global_device_ids=true | all-gather | bytes 1376256 | tf_op jit(solution)/shard_map/all_gather | solution.py:131
  21.5 5.0 %collective-permute-done = bf16[128,1792]{1,0:T(8,128)(2,1)S(1)} collective-permute-done((bf16[128,1792]{1,0:T(8,128)(2,1)}, bf16[128,1792]{1,0:T(8,128)(2,1)S(1)}, u32[]{:S(2)}, u32[]{:S(2)}) %collective-permute-start) | collective-permute-done | bytes 458784 | tf_op jit(solution)/shard_map/ppermute | solution.py:10
  26.5 2.5 %all_gather.9 = bf16[128,3584]{1,0:T(8,128)(2,1)S(1)} all-gather(bf16[128,1792]{1,0:T(8,128)(2,1)S(1)} %collective-permute-done), channel_id=1, replica_groups=mesh['pipe'=4,'expert'=4,'tensor'=2] {'tensor'}, dimensions={1}, use_global_device_ids=true | all-gather | bytes 1376256 | tf_op jit(solution)/shard_map/all_gather | solution.py:130
  31.1 4.1 %all-to-all-start = ((bf16[3,4,4,3584]{3,2,0,1:T(4,128)(2,1)}), bf16[3,4,4,3584]{3,2,0,1:T(4,128)(2,1)}, u32[]{:S(2)}, u32[]{:S(2)}) async-start(bf16[3,4,4,3584]{3,2,0,1:T(4,128)(2,1)} %bitcast.11), calls=%async_computation | async-start | bytes 688128 | tf_op jit(solution)/shard_map/all_to_all | solution.py:143
  35.2 3.6 %fusion.3 = f32[128,512]{1,0:T(8,128)S(1)} fusion(bf16[128,3584]{1,0:T(8,128)(2,1)} %copy-done.2, bf16[1,512,3584]{2,1,0:T(8,128)(2,1)} %param.25), kind=kOutput, calls=%fused_computation.10 | convolution fusion | flops 469762048 | bytes 4849664 | tf_op jit(solution)/shard_map/dot_general | solution.py:23
  38.8 6.6 %fusion.11 = f32[128,3584]{1,0:T(8,128)} fusion(bf16[1,3584,512]{2,1,0:T(8,128)(2,1)} %param.23, f32[128,512]{1,0:T(8,128)S(1)} %fusion.3, bf16[1,3584,512]{2,1,0:T(8,128)(2,1)} %param.24, bf16[1,128,3584]{2,1,0:T(8,128)(2,1)} %copy-done.1, f32[128,512]{1,0:T(8,128)S(1)} %fusion.13), kind=kOutput, calls=%fused_computation.18 | convolution fusion | flops 940179456 | bytes 10616832 | tf_op jit(solution)/shard_map/dot_general | solution.py:23
  45.3 1.8 %fusion.112 = (bf16[1,4,4,3584]{3,2,0,1:T(4,128)(2,1)S(1)}, bf16[1,4,4,3584]{3,2,0,1:T(4,128)(2,1)}, bf16[1,4,4,3584]{3,2,0,1:T(4,128)(2,1)}) fusion(bf16[3,4,4,3584]{3,2,0,1:T(4,128)(2,1)} %all-to-all-done), kind=kLoop, calls=%fused_computation.129 | loop fusion | bytes 688128 | tf_op jit(solution)/shard_map/slice | solution.py:145
  48.1 1.8 %fusion.29 = f32[16,256]{1,0:T(8,128)S(1)} fusion(bf16[16,3584]{1,0:T(8,128)(2,1)S(1)} %squeeze.52, bf16[1,1,3584,256]{3,2,1,0:T(8,128)(2,1)} %param.20), kind=kOutput, calls=%fused_computation.36 | convolution fusion | flops 29360128 | bytes 1966080 | tf_op jit(solution)/shard_map/dot_general | solution.py:69
  49.9 3.3 %convolution_convert_fusion = bf16[16,3584]{1,0:T(8,128)(2,1)} fusion(bf16[1,1,256,3584]{3,2,1,0:T(8,128)(2,1)} %param.22, bf16[16,3584]{1,0:T(8,128)(2,1)S(1)} %squeeze.52, bf16[1,1,3584,256]{3,2,1,0:T(8,128)(2,1)S(1)} %copy-done, f32[16,256]{1,0:T(8,128)S(1)} %fusion.29), kind=kOutput, calls=%fused_computation.5 | convolution fusion | flops 58802176 | bytes 3915776 | tf_op jit(solution)/shard_map/dot_general | solution.py:72
  55.8 2.1 %fusion.17 = f32[16,256]{1,0:T(8,128)S(1)} fusion(bf16[16,3584]{1,0:T(8,128)(2,1)S(1)} %squeeze.56, bf16[1,1,256,3584]{3,2,1,0:T(8,128)(2,1)} %param.22), kind=kOutput, calls=%fused_computation.24 | convolution fusion | flops 29360128 | bytes 1966080 | tf_op jit(solution)/shard_map/dot_general | solution.py:23
  57.9 1.8 %fusion.27 = f32[16,256]{1,0:T(8,128)S(1)} fusion(bf16[16,3584]{1,0:T(8,128)(2,1)S(1)} %squeeze.57, bf16[1,1,3584,256]{3,2,1,0:T(8,128)(2,1)} %param.20), kind=kOutput, calls=%fused_computation.34 | convolution fusion | flops 29360128 | bytes 1966080 | tf_op jit(solution)/shard_map/dot_general | solution.py:73
  59.8 3.5 %fusion.25 = f32[16,3584]{1,0:T(8,128)} fusion(bf16[1,1,3584,256]{3,2,1,0:T(8,128)(2,1)} %param.20, f32[16,256]{1,0:T(8,128)S(1)} %fusion.17, bf16[16,3584]{1,0:T(8,128)(2,1)S(1)} %squeeze.57, bf16[1,1,3584,256]{3,2,1,0:T(8,128)(2,1)S(1)} %copy-done, f32[16,256]{1,0:T(8,128)S(1)} %fusion.27), kind=kOutput, calls=%fused_computation.32 | convolution fusion | flops 58761216 | bytes 4046848 | tf_op jit(solution)/shard_map/dot_general | solution.py:23
  63.2 2.2 %fusion.1 = bf16[16,3584]{1,0:T(8,128)(2,1)} fusion(f32[16,3584]{1,0:T(8,128)} %fusion.25, bf16[1,1,3584,256]{3,2,1,0:T(8,128)(2,1)S(1)} %copy-done, f32[16,256]{1,0:T(8,128)S(1)} %fusion.17, f32[16,256]{1,0:T(8,128)S(1)} %fusion.27), kind=kOutput, calls=%fused_computation.4 | convolution fusion | flops 29499392 | bytes 2211840 | tf_op jit(solution)/shard_map/dot_general | solution.py:23
  65.4 1.6 %stack.41 = bf16[1,4,4,3584]{3,2,1,0:T(4,128)(2,1)} reshape(bf16[16,3584]{1,0:T(8,128)(2,1)} %fusion.1) | data formatting | bytes 229376 | tf_op jit(solution)/shard_map/stack | solution.py:150
  69.0 4.1 %all-to-all-start.1 = ((bf16[4,2,1,4,3584]{4,3,1,2,0:T(4,128)(2,1)}), bf16[4,2,1,4,3584]{4,3,1,2,0:T(4,128)(2,1)}, u32[]{:S(2)}, u32[]{:S(2)}) async-start(bf16[4,2,1,4,3584]{4,3,1,2,0:T(4,128)(2,1)} %pad_maximum_fusion), calls=%async_computation.1 | async-start | bytes 458752 | tf_op jit(solution)/shard_map/all_to_all | solution.py:147
  73.1 2.7 %fusion.9 = f32[128,512]{1,0:T(8,128)S(1)} fusion(bf16[128,3584]{1,0:T(8,128)(2,1)S(1)} %all_gather.9, bf16[1,3584,512]{2,1,0:T(8,128)(2,1)} %param.24), kind=kOutput, calls=%fused_computation.16 | convolution fusion | flops 469762048 | bytes 4849664 | tf_op jit(solution)/shard_map/dot_general | solution.py:86
  75.8 2.9 %all-to-all-done.1 = bf16[4,2,1,4,3584]{4,3,1,2,0:T(4,128)(2,1)} async-done(((bf16[4,2,1,4,3584]{4,3,1,2,0:T(4,128)(2,1)}), bf16[4,2,1,4,3584]{4,3,1,2,0:T(4,128)(2,1)}, u32[]{:S(2)}, u32[]{:S(2)}) %all-to-all-start.1) | async-done | bytes 229408 | tf_op jit(solution)/shard_map/all_to_all | solution.py:147
  78.7 1.7 %fusion.113 = (bf16[1,4,1,4,3584]{4,3,0,2,1:T(4,128)(2,1)}, bf16[1,4,1,4,3584]{4,3,0,2,1:T(4,128)(2,1)}) fusion(bf16[2,4,1,4,3584]{4,3,0,2,1:T(4,128)(2,1)} %bitcast.19), kind=kLoop, calls=%fused_computation.130 | loop fusion | bytes 458752 | tf_op jit(solution)/shard_map/slice | solution.py:171
  80.4 1.6 %squeeze.58 = bf16[16,3584]{1,0:T(8,128)(2,1)} reshape(bf16[1,4,1,4,3584]{4,3,0,2,1:T(4,128)(2,1)} %get-tuple-element.10) | data formatting | bytes 229376 | tf_op jit(solution)/shard_map/squeeze | solution.py:170
  82.0 2.6 %fusion.71 = f32[128,3584]{1,0:T(8,128)} fusion(bf16[16,3584]{1,0:T(8,128)(2,1)} %squeeze.58, bf16[16,128]{1,0:T(8,128)(2,1)S(1)} %bitcast.134, bf16[16,128]{1,0:T(8,128)(2,1)S(1)} %bitcast.135), kind=kOutput, calls=%fused_computation.61 | convolution fusion | flops 29835264 | bytes 1957888 | tf_op jit(solution)/shard_map/dot_general | solution.py:52
  84.7 6.2 %convolution_add_fusion.1 = f32[128,3584]{1,0:T(8,128)} fusion(f32[128,3584]{1,0:T(8,128)} %fusion.71, bf16[1,512,3584]{2,1,0:T(8,128)(2,1)} %param.25, f32[128,512]{1,0:T(8,128)S(1)} %fusion.9, bf16[128,3584]{1,0:T(8,128)(2,1)S(1)} %all_gather.9, bf16[1,3584,512]{2,1,0:T(8,128)(2,1)} %param.23), kind=kOutput, calls=%fused_computation.2 | convolution fusion | flops 940376064 | bytes 12189696 | tf_op jit(solution)/shard_map/dot_general | solution.py:88
  90.9 2.2 %constant_dynamic-slice_fusion = f32[128,1792]{1,0:T(8,128)} fusion(f32[128,3584]{1,0:T(8,128)} %convolution_add_fusion.1, s32[]{:T(128)S(6)} %select_n.74), kind=kLoop, calls=%fused_computation.119 | loop fusion | bytes 1835012 | tf_op jit(solution)/shard_map/dynamic_slice | solution.py:63
  93.6 1.1 %copy-done.5 = f32[128,3584]{1,0:T(8,128)S(1)} copy-done((f32[128,3584]{1,0:T(8,128)S(1)}, f32[128,3584]{1,0:T(8,128)}, u32[]{:S(2)}) %copy-start.5) | copy-done | bytes 1835032
  94.6 3.3 %fusion = f32[128,3584]{1,0:T(8,128)S(1)} fusion(f32[128,3584]{1,0:T(8,128)S(1)} %fusion.114, f32[128,3584]{1,0:T(8,128)S(1)} %copy-done.5, bf16[1,3584,512]{2,1,0:T(8,128)(2,1)} %param.24, f32[128,512]{1,0:T(8,128)S(1)} %fusion.3, f32[128,512]{1,0:T(8,128)S(1)} %fusion.13), kind=kOutput, calls=%fused_computation.1 | convolution fusion | flops 471072768 | bytes 9699328 | tf_op jit(solution)/shard_map/dot_general | solution.py:23
  98.0 1.2 %copy-done.3 = f32[128,3584]{1,0:T(8,128)} copy-done((f32[128,3584]{1,0:T(8,128)}, f32[128,3584]{1,0:T(8,128)S(1)}, u32[]{:S(2)}) %copy-start.3) | copy-done | bytes 1835032
  99.2 1.0 constant_dynamic-slice_fusion.1
  100.8 2.2 %fusion.65 = bf16[1,128,1792]{2,1,0:T(8,128)(2,1)} fusion(f32[128,1792]{1,0:T(8,128)S(1)} %collective-permute-done.2, f32[128,3584]{1,0:T(8,128)} %convolution_add_fusion.1, s32[]{:T(128)S(6)} %select_n.72), kind=kLoop, calls=%fused_computation.51 | loop fusion | flops 458752 | bytes 2293764 | tf_op jit(solution)/shard_map/broadcast_in_dim | solution.py:177
  103.2 2.0 %fusion.66 = bf16[1,128,1792]{2,1,0:T(8,128)(2,1)} fusion(f32[128,1792]{1,0:T(8,128)} %collective-permute-done.3, f32[128,3584]{1,0:T(8,128)S(1)} %copy-done.4, s32[]{:T(128)S(6)} %select_n.72), kind=kLoop, calls=%fused_computation.52 | loop fusion | flops 458752 | bytes 2293764 | tf_op jit(solution)/shard_map/broadcast_in_dim | solution.py:177
  (48 shorter events, 12.0 us)
Async XLA Ops:
  0.6 49.3 %copy-start = (bf16[1,1,3584,256]{3,2,1,0:T(8,128)(2,1)S(1)}, bf16[1,1,3584,256]{3,2,1,0:T(8,128)(2,1)}, u32[]{:S(2)}) copy-start(bf16[1,1,3584,256]{3,2,1,0:T(8,128)(2,1)} %param.21) | copy-start | bytes 5505028
  0.6 16.4 %collective-permute-start.1 = (bf16[128,1792]{1,0:T(8,128)(2,1)}, bf16[128,1792]{1,0:T(8,128)(2,1)}, u32[]{:S(2)}, u32[]{:S(2)}) collective-permute-start(bf16[128,1792]{1,0:T(8,128)(2,1)} %bitcast.138), channel_id=1, source_target_pairs={{8,0},{16,8},{24,16},{0,24},{9,1},{17,9},{25,17},{1,25},{10,2},{18... | collective-permute-start | bytes 1376264 | tf_op jit(solution)/shard_map/ppermute | solution.py:10
  5.8 20.7 %collective-permute-start = (bf16[128,1792]{1,0:T(8,128)(2,1)}, bf16[128,1792]{1,0:T(8,128)(2,1)S(1)}, u32[]{:S(2)}, u32[]{:S(2)}) collective-permute-start(bf16[128,1792]{1,0:T(8,128)(2,1)} %bitcast.139), channel_id=1, source_target_pairs={{24,0},{0,8},{8,16},{16,24},{25,1},{1,9},{9,17},{17,25},{26,2},{2,... | collective-permute-start | bytes 1376264 | tf_op jit(solution)/shard_map/ppermute | solution.py:10
  9.5 3.0 %copy-start.1 = (bf16[1,128,3584]{2,1,0:T(8,128)(2,1)}, bf16[1,128,3584]{2,1,0:T(8,128)(2,1)S(1)}, u32[]{:S(2)}) copy-start(bf16[1,128,3584]{2,1,0:T(8,128)(2,1)S(1)} %all-gather) | copy-start | bytes 2752516
  19.7 0.9 copy-start.2
  31.1 14.3 %all-to-all-start = ((bf16[3,4,4,3584]{3,2,0,1:T(4,128)(2,1)}), bf16[3,4,4,3584]{3,2,0,1:T(4,128)(2,1)}, u32[]{:S(2)}, u32[]{:S(2)}) async-start(bf16[3,4,4,3584]{3,2,0,1:T(4,128)(2,1)} %bitcast.11), calls=%async_computation | async-start | bytes 688128 | tf_op jit(solution)/shard_map/all_to_all | solution.py:143
  63.2 3.8 %copy-start.6 = (bf16[2,4,4,3584]{3,2,1,0:T(4,128)(2,1)S(1)}, bf16[2,4,4,3584]{3,2,1,0:T(4,128)(2,1)}, u32[]{:S(2)}) copy-start(bf16[2,4,4,3584]{3,2,1,0:T(4,128)(2,1)} %constant_dynamic-update-slice_fusion.1) | copy-start | bytes 688132
  69.0 9.8 %all-to-all-start.1 = ((bf16[4,2,1,4,3584]{4,3,1,2,0:T(4,128)(2,1)}), bf16[4,2,1,4,3584]{4,3,1,2,0:T(4,128)(2,1)}, u32[]{:S(2)}, u32[]{:S(2)}) async-start(bf16[4,2,1,4,3584]{4,3,1,2,0:T(4,128)(2,1)} %pad_maximum_fusion), calls=%async_computation.1 | async-start | bytes 458752 | tf_op jit(solution)/shard_map/all_to_all | solution.py:147
  90.9 2.2 %copy-start.7 = (bf16[1,4,1,4,3584]{4,3,0,2,1:T(4,128)(2,1)S(1)}, bf16[1,4,1,4,3584]{4,3,0,2,1:T(4,128)(2,1)}, u32[]{:S(2)}) copy-start(bf16[1,4,1,4,3584]{4,3,0,2,1:T(4,128)(2,1)} %get-tuple-element.9) | copy-start | bytes 344068
  93.1 7.7 %collective-permute-start.2 = (f32[128,1792]{1,0:T(8,128)}, f32[128,1792]{1,0:T(8,128)S(1)}, u32[]{:S(2)}, u32[]{:S(2)}) collective-permute-start(f32[128,1792]{1,0:T(8,128)} %constant_dynamic-slice_fusion), channel_id=1, source_target_pairs={{1,0},{0,1},{3,2},{2,3},{5,4},{4,5},{7,6},{6,7},{9,8},{8,9},{11,10... | collective-permute-start | bytes 2752520 | tf_op jit(solution)/shard_map/ppermute | solution.py:10
  93.1 1.5 %copy-start.5 = (f32[128,3584]{1,0:T(8,128)S(1)}, f32[128,3584]{1,0:T(8,128)}, u32[]{:S(2)}) copy-start(f32[128,3584]{1,0:T(8,128)} %fusion.11) | copy-start | bytes 5505028
  98.0 1.3 %copy-start.3 = (f32[128,3584]{1,0:T(8,128)}, f32[128,3584]{1,0:T(8,128)S(1)}, u32[]{:S(2)}) copy-start(f32[128,3584]{1,0:T(8,128)S(1)} %fusion) | copy-start | bytes 5505028
  100.2 3.0 %collective-permute-start.3 = (f32[128,1792]{1,0:T(8,128)}, f32[128,1792]{1,0:T(8,128)}, u32[]{:S(2)}, u32[]{:S(2)}) collective-permute-start(f32[128,1792]{1,0:T(8,128)} %constant_dynamic-slice_fusion.1), channel_id=1, source_target_pairs={{1,0},{0,1},{3,2},{2,3},{5,4},{4,5},{7,6},{6,7},{9,8},{8,9},{11,10... | collective-permute-start | bytes 2752520 | tf_op jit(solution)/shard_map/ppermute | solution.py:10
  100.7 2.4 %copy-start.4 = (f32[128,3584]{1,0:T(8,128)S(1)}, f32[128,3584]{1,0:T(8,128)}, u32[]{:S(2)}) copy-start(f32[128,3584]{1,0:T(8,128)} %copy-done.3) | copy-start | bytes 5505028
